TPU v7x, 32 devices: a whole 2x2x4 slice. The times are simulated.
32 devices in a mesh: dp: 8 (over y, x, core), seq: 4 (over z).
Axes of the slice: x: 2, y: 2, z: 4, core: 2. Of those that a mesh axis runs over, the one named last changes fastest.
Arguments:
- inputs: bfloat16 [24, 1024, 768], P('dp', 'seq'), may hold values from -6 to 6
- segments: int32 [24, 1024], P('dp'), may hold values from 0 to 3, never falling along the last dimension, each value on 1 to 512 neighbouring positions
- cotangent: bfloat16 [24, 1024, 768], P('dp', 'seq'), may hold values from -6 to 6
- weights: float32 [768, 9216], P(None, 'dp'), may hold values from -0.18042196 to 0.18042196
- first_moment: float32 [768, 9216], P(None, 'dp'), may hold values from -112 to 112
- second_moment: float32 [768, 9216], P(None, 'dp'), may hold values from 12.288 to 98.304
- bases: float32 [4, 768, 768], replicated, may hold values from -0.08660254 to 0.8866025
- right_bases: float32 [9216, 3072], P('dp'), may hold values from -0.08660254 to 0.8866025, as said below
- small: float32 [9216], replicated, may hold values from -2 to 2
- small_first: float32 [9216], replicated, may hold values from -112 to 112
- small_second: float32 [9216], replicated, may hold values from 12.288 to 98.304
Outputs:
- output: bfloat16 [24, 1024, 768], P('dp', 'seq')
- input_grad: bfloat16 [24, 1024, 768], P('dp', 'seq')
- weight_grad: float32 [768, 9216], P(None, 'dp')
- first_new: float32 [768, 9216], P(None, 'dp')
- second_new: float32 [768, 9216], P(None, 'dp')
- weights_new: float32 [768, 9216], P(None, 'dp')
- weights_low: bfloat16 [768, 9216], P(None, 'dp')
- small_grad: float32 [9216], replicated
- small_first_new: float32 [9216], replicated
- small_second_new: float32 [9216], replicated
- small_new: float32 [9216], replicated
Inputs may be any that keep to these rules, and one draw needn't show every extreme that they name: `segments`: along each row the ids never fall; every id covers 1 to 512 positions and one covers exactly 512. `right_bases`: entries of a row past the number of columns of that row's block are zero.
All inputs are finite; a program needn't handle non-finite values.
Results may differ from a plain program's by a relative error of at most 0.012.
Values may be sent and summed in bfloat16 or wider, within the bound.
A program may use at most 256 MiB of HBM per device.

v0:
```python
import jax
import jax.numpy as jnp
from jax import lax
from jax.sharding import PartitionSpec as P

D = 768
HEADS = 12
HD = 64
FF = 3072
STEP = 10
highest = lax.Precision.HIGHEST
norm_eps = 1e-12
beta_first = 0.9
beta_second = 0.999
adam_eps = 1e-08
learn_rate = 0.03
small_rate = 0.3


def contract_first(left, right):
    return lax.dot_general(
        left, right, (((0,), (0,)), ((), ())), preferred_element_type=jnp.float32
    )


def contract_last(left, right):
    return lax.dot_general(
        left, right, (((1,), (1,)), ((), ())), preferred_element_type=jnp.float32
    )


def exact_last(left, right):
    return lax.dot_general(
        left, right, (((1,), (1,)), ((), ())), precision=highest, preferred_element_type=jnp.float32
    )


def normalize(resid, gain, shift):
    centre = resid - jnp.mean(resid, axis=-1, keepdims=True)
    spread = jnp.mean(centre * centre, axis=-1, keepdims=True)
    inv_std = lax.rsqrt(spread + norm_eps)
    scaled = centre * inv_std
    return (scaled * gain + shift, scaled, inv_std)


def norm_back(grad, scaled, inv_std, gain):
    lifted = grad * gain
    return inv_std * (
        lifted
        - jnp.mean(lifted, axis=-1, keepdims=True)
        - scaled * jnp.mean(lifted * scaled, axis=-1, keepdims=True)
    )


def moments(grad, first, second):
    first_out = beta_first * first + (1.0 - beta_first) * grad
    second_out = beta_second * second + (1.0 - beta_second) * grad * grad
    heading = (
        first_out
        / (1.0 - beta_first**STEP)
        / (jnp.sqrt(second_out / (1.0 - beta_second**STEP)) + adam_eps)
    )
    return (first_out, second_out, heading)


def on_device(
    inputs,
    segments,
    cotangent,
    weights,
    first_moment,
    second_moment,
    bases,
    right_bases,
    small,
    small_first,
    small_second,
):
    number, quarter, width = inputs.shape
    length = segments.shape[1]
    groups = lax.axis_size("seq")
    owners = lax.axis_size("dp")
    heads_local = HEADS // groups
    group_width = width // groups
    scale = HD ** (-0.5)
    share = weights.shape[1]
    block_widths = [3 * D // owners, D // owners, FF // owners, FF // owners]
    block_starts = [
        0,
        block_widths[0],
        block_widths[0] + block_widths[1],
        block_widths[0] + block_widths[1] + block_widths[2],
    ]

    def split_wide(matrix):
        shaped = matrix.reshape(matrix.shape[0], owners, share)
        return [
            shaped[:, :, block_starts[which] : block_starts[which] + block_widths[which]].reshape(
                matrix.shape[0], owners * block_widths[which]
            )
            for which in range(4)
        ]

    def join_wide(parts):
        rows = parts[0].shape[0]
        return jnp.concatenate(
            [parts[which].reshape(rows, owners, block_widths[which]) for which in range(4)], axis=2
        ).reshape(rows, owners * share)

    wide = lax.all_gather(weights.astype(jnp.bfloat16), "dp", axis=1, tiled=True)
    w_qkv, w_out, w_up, w_down = split_wide(wide)
    pieces = [small[index * D : (index + 1) * D] for index in range(8)] + [small[8 * D :]]
    (
        gain_one,
        gain_two,
        shift_one,
        shift_two,
        bias_query,
        bias_value,
        bias_out,
        bias_down,
        bias_up,
    ) = pieces
    token_rows = inputs.reshape(number * quarter, width)
    acts = token_rows.astype(jnp.float32)
    project = jnp.dot(token_rows, w_qkv, preferred_element_type=jnp.float32)
    queries = (project[:, :D] + bias_query).astype(jnp.bfloat16)
    keys_all = project[:, D : 2 * D].astype(jnp.bfloat16)
    values = (project[:, 2 * D :] + bias_value).astype(jnp.bfloat16)

    def to_heads(array):
        return array.reshape(number, quarter, groups, group_width)

    head_q, head_k, head_v = (
        lax.all_to_all(to_heads(queries), "seq", split_axis=2, concat_axis=1, tiled=True),
        lax.all_to_all(to_heads(keys_all), "seq", split_axis=2, concat_axis=1, tiled=True),
        lax.all_to_all(to_heads(values), "seq", split_axis=2, concat_axis=1, tiled=True),
    )
    head_q = head_q.reshape(number, length, heads_local, HD)
    head_k = head_k.reshape(number, length, heads_local, HD)
    head_v = head_v.reshape(number, length, heads_local, HD)

    def attend_one(item):
        one_q, one_k, one_v, marks = item
        same = (marks[:, None] == marks[None, :])[None]
        raw = jnp.einsum("qhd,khd->hqk", one_q, one_k, preferred_element_type=jnp.float32) * scale
        masked = jnp.where(same, raw, -1e30)
        peak = jnp.max(masked, axis=-1, keepdims=True)
        expo = jnp.exp(masked - peak)
        totals = jnp.sum(expo, axis=-1, keepdims=True)
        probs = expo / totals
        log_sum = peak + jnp.log(totals)
        mixed = jnp.einsum(
            "hqk,khd->qhd", probs.astype(jnp.bfloat16), one_v, preferred_element_type=jnp.float32
        )
        return (mixed.astype(jnp.bfloat16), log_sum)

    mixed, log_sums = lax.map(attend_one, (head_q, head_k, head_v, segments))
    context_heads = mixed.reshape(number, length, 1, group_width)
    context = lax.all_to_all(context_heads, "seq", split_axis=1, concat_axis=2, tiled=True).reshape(
        number * quarter, width
    )
    attended = jnp.dot(context, w_out, preferred_element_type=jnp.float32) + bias_out
    first, scaled_one, inv_one = normalize(acts + attended, gain_one, shift_one)
    first_low = first.astype(jnp.bfloat16)
    upward = jnp.dot(first_low, w_up, preferred_element_type=jnp.float32) + bias_up
    active_full, gelu_pull = jax.vjp(lambda value: jax.nn.gelu(value, approximate=False), upward)
    active = active_full.astype(jnp.bfloat16)
    downward = contract_last(active, w_down) + bias_down
    output, scaled_two, inv_two = normalize(first + downward, gain_two, shift_two)
    grad_out = cotangent.reshape(number * quarter, width).astype(jnp.float32)
    d_two = norm_back(grad_out, scaled_two, inv_two, gain_two)
    grad_gain_two = jnp.sum(grad_out * scaled_two, axis=0)
    grad_shift_two = jnp.sum(grad_out, axis=0)
    d_down = d_two.astype(jnp.bfloat16)
    grad_bias_down = jnp.sum(d_down.astype(jnp.float32), axis=0)
    grad_w_down = contract_first(d_down, active)
    d_active = jnp.dot(d_down, w_down, preferred_element_type=jnp.float32)
    (d_up_full,) = gelu_pull(d_active)
    d_up = d_up_full.astype(jnp.bfloat16)
    grad_bias_up = jnp.sum(d_up.astype(jnp.float32), axis=0)
    grad_w_up = contract_first(first_low, d_up)
    d_first = d_two + contract_last(d_up, w_up)
    d_one = norm_back(d_first, scaled_one, inv_one, gain_one)
    grad_gain_one = jnp.sum(d_first * scaled_one, axis=0)
    grad_shift_one = jnp.sum(d_first, axis=0)
    d_att = d_one.astype(jnp.bfloat16)
    grad_bias_out = jnp.sum(d_att.astype(jnp.float32), axis=0)
    grad_w_out = contract_first(context, d_att)
    d_context = contract_last(d_att, w_out).astype(jnp.bfloat16)
    d_heads = lax.all_to_all(
        to_heads(d_context), "seq", split_axis=2, concat_axis=1, tiled=True
    ).reshape(number, length, heads_local, HD)

    def attend_back(item):
        one_q, one_k, one_v, marks, one_grad, one_log = item
        same = (marks[:, None] == marks[None, :])[None]
        raw = jnp.einsum("qhd,khd->hqk", one_q, one_k, preferred_element_type=jnp.float32) * scale
        again = jnp.where(same, jnp.exp(raw - one_log), 0.0)
        d_values = jnp.einsum(
            "hqk,qhd->khd", again.astype(jnp.bfloat16), one_grad, preferred_element_type=jnp.float32
        )
        d_probs = jnp.einsum("qhd,khd->hqk", one_grad, one_v, preferred_element_type=jnp.float32)
        d_scores = (again * (d_probs - jnp.sum(again * d_probs, axis=-1, keepdims=True))).astype(
            jnp.bfloat16
        )
        d_queries = (
            jnp.einsum("hqk,khd->qhd", d_scores, one_k, preferred_element_type=jnp.float32) * scale
        )
        d_keys = (
            jnp.einsum("hqk,qhd->khd", d_scores, one_q, preferred_element_type=jnp.float32) * scale
        )
        return (
            d_queries.astype(jnp.bfloat16),
            d_keys.astype(jnp.bfloat16),
            d_values.astype(jnp.bfloat16),
        )

    grads_q, grads_k, grads_v = lax.map(
        attend_back, (head_q, head_k, head_v, segments, d_heads, log_sums)
    )

    def to_send(array):
        return array.reshape(number, length, 1, group_width)

    back_q, back_k, back_v = (
        lax.all_to_all(to_send(grads_q), "seq", split_axis=1, concat_axis=2, tiled=True),
        lax.all_to_all(to_send(grads_k), "seq", split_axis=1, concat_axis=2, tiled=True),
        lax.all_to_all(to_send(grads_v), "seq", split_axis=1, concat_axis=2, tiled=True),
    )
    d_project = jnp.concatenate(
        [
            back_q.reshape(number * quarter, width),
            back_k.reshape(number * quarter, width),
            back_v.reshape(number * quarter, width),
        ],
        axis=1,
    )
    grad_bias_query = jnp.sum(back_q.reshape(number * quarter, width).astype(jnp.float32), axis=0)
    grad_bias_value = jnp.sum(back_v.reshape(number * quarter, width).astype(jnp.float32), axis=0)
    grad_w_qkv = contract_first(token_rows, d_project)
    input_grad = (d_one + contract_last(d_project, w_qkv)).astype(jnp.bfloat16)
    grad_full = join_wide([grad_w_qkv, grad_w_out, grad_w_up, grad_w_down])
    small_local = jnp.concatenate(
        [
            grad_gain_one,
            grad_gain_two,
            grad_shift_one,
            grad_shift_two,
            grad_bias_query,
            grad_bias_value,
            grad_bias_out,
            grad_bias_down,
            grad_bias_up,
        ]
    )
    small_grad = lax.psum(small_local, ("dp", "seq"))
    reduced = lax.psum_scatter(grad_full, "dp", scatter_dimension=1, tiled=True)
    reduced = lax.psum(reduced.astype(jnp.bfloat16), "seq").astype(jnp.float32)
    right_rows = []
    turned_parts = []
    for which in range(4):
        begin = block_starts[which]
        count = block_widths[which]
        extent = owners * count
        rows_here = right_bases[begin : begin + count, :extent]
        right_rows.append(rows_here)
        left_turned = jnp.dot(bases[which].T, reduced[:, begin : begin + count], precision=highest)
        turned_parts.append(jnp.dot(left_turned, rows_here, precision=highest))
    term = join_wide(turned_parts)
    rotated = lax.psum_scatter(term, "dp", scatter_dimension=1, tiled=True)
    first_new, second_new, heading = moments(rotated, first_moment, second_moment)
    left_step = jnp.concatenate(
        [
            jnp.dot(
                bases[which],
                heading[:, block_starts[which] : block_starts[which] + block_widths[which]],
                precision=highest,
            )
            for which in range(4)
        ],
        axis=1,
    )
    every_step = lax.all_gather(left_step.astype(jnp.bfloat16), "dp", axis=1, tiled=True).astype(
        left_step.dtype
    )
    step_parts = split_wide(every_step)
    update = jnp.concatenate(
        [exact_last(step_parts[which], right_rows[which]) for which in range(4)], axis=1
    )
    weights_new = weights - learn_rate * update
    small_first_new, small_second_new, small_heading = moments(
        small_grad, small_first, small_second
    )
    small_new = small - small_rate * small_heading
    return (
        output.astype(jnp.bfloat16).reshape(number, quarter, width),
        input_grad.reshape(number, quarter, width),
        reduced,
        first_new,
        second_new,
        weights_new,
        weights_new.astype(jnp.bfloat16),
        small_grad,
        small_first_new,
        small_second_new,
        small_new,
    )


def solution(mesh):
    return jax.shard_map(
        on_device,
        mesh=mesh,
        in_specs=(
            P("dp", "seq", None),
            P("dp", None),
            P("dp", "seq", None),
            P(None, "dp"),
            P(None, "dp"),
            P(None, "dp"),
            P(),
            P("dp", None),
            P(),
            P(),
            P(),
        ),
        out_specs=(
            P("dp", "seq", None),
            P("dp", "seq", None),
            P(None, "dp"),
            P(None, "dp"),
            P(None, "dp"),
            P(None, "dp"),
            P(None, "dp"),
            P(),
            P(),
            P(),
            P(),
        ),
        check_vma=False,
    )
```

profile of v0, /device:TPU:0, one launch (start us, length us, event | category | flops | bytes accessed | tf_op | source)
XLA Modules:
  0.0 1506.3 jit_solution(18342674644949686309)
XLA Ops:
  11.3 80.8 %all-gather.3.cloned.1.call-done = bf16[768,9216]{1,0:T(8,128)(2,1)} async-done(((bf16[768,1152]{1,0:T(8,128)(2,1)}), bf16[768,9216]{1,0:T(8,128)(2,1)}) %all-gather.3.cloned.1.call-update) | async-done | bytes 14155792 | tf_op jit(solution)/shard_map/all_gather | solution.py:110
  92.1 18.5 %copy.112 = bf16[768,9216]{0,1:T(8,128)(2,1)} copy(bf16[768,9216]{1,0:T(8,128)(2,1)} %all-gather.3.cloned.1.call-done) | data formatting | bytes 28311552 | tf_op jit(solution)/shard_map/all_gather | solution.py:110
  132.9 23.3 %all-to-all-done = bf16[3,256,4,192]{1,3,0,2:T(8,128)(2,1)S(1)} async-done(((bf16[3,256,4,192]{1,3,0,2:T(8,128)(2,1)}), bf16[3,256,4,192]{1,3,0,2:T(8,128)(2,1)S(1)}, u32[]{:S(2)}, u32[]{:S(2)}) %all-to-all-start) | async-done | bytes 1179680 | tf_op jit(solution)/shard_map/all_to_all | solution.py:137
  168.9 19.7 %all-to-all-done.1 = bf16[3,256,4,192]{1,3,0,2:T(8,128)(2,1)} async-done(((bf16[3,256,4,192]{1,3,0,2:T(8,128)(2,1)}), bf16[3,256,4,192]{1,3,0,2:T(8,128)(2,1)}, u32[]{:S(2)}, u32[]{:S(2)}) %all-to-all-start.1) | async-done | bytes 1179680 | tf_op jit(solution)/shard_map/all_to_all | solution.py:135
  201.9 18.8 %all-to-all-done.2 = bf16[3,256,4,192]{1,3,0,2:T(8,128)(2,1)S(1)} async-done(((bf16[3,256,4,192]{1,3,0,2:T(8,128)(2,1)}), bf16[3,256,4,192]{1,3,0,2:T(8,128)(2,1)S(1)}, u32[]{:S(2)}, u32[]{:S(2)}) %all-to-all-start.2) | async-done | bytes 1179680 | tf_op jit(solution)/shard_map/all_to_all | solution.py:136
  224.5 47.5 %while.26 = (s32[]{:T(128)}, bf16[3,1024,3,64]{1,3,2,0:T(8,128)(2,1)}, f32[3,3,1024,1]{2,1,3,0:T(4,128)}, bf16[3,1024,3,64]{1,3,2,0:T(8,128)(2,1)}, s32[3,1024]{...) while((s32[]{:T(128)}, ...), condition=%wide.region_3.4_spmd, body=%wide.region_0.3_spmd.sunk | while | flops 844297216 | bytes 47827072 | solution.py:158
  284.9 8.2 fusion.168
  293.1 35.5 %all-to-all-done.3 = bf16[3,1024,1,192]{3,0,2,1:T(4,128)(2,1)} async-done(((bf16[3,1024,1,192]{3,0,2,1:T(4,128)(2,1)}), bf16[3,1024,1,192]{3,0,2,1:T(4,128)(2,1)}, u32[]{:S(2)}, u32[]{:S(2)}) %all-to-all-start.3) | async-done | bytes 1179680 | tf_op jit(solution)/shard_map/all_to_all | solution.py:160
  342.1 28.3 %multiply_convert_fusion.1 = (bf16[768,3072]{1,0:T(8,128)(2,1)S(1)}, f32[768,3072]{1,0:T(8,128)}, f32[768,3072]{1,0:T(8,128)}) fusion(f32[3072]{0:T(1024)S(1)} %slice.124, bf16[768,3072]{0,1:T(8,128)(2,1)} %bitcast.308, f32[768,768]{1,0:T(8,128)S(1)} %get-tuple-element.239, f32[768]{0:T(1024)S(1)} %copy-done.32, f32[768]{0:T(1024)S(1)} %copy-done.28, ...), kind=kOutput, calls=%fused_computation.70 | convolution fusion | flops 3782541312 | bytes 30695424 | tf_op jit(solution)/shard_map/dot_general | solution.py:166
  379.0 13.2 convert_reduce_fusion
  404.9 30.7 %all_to_all.120 = bf16[3,256,4,192]{1,3,0,2:T(8,128)(2,1)S(1)} all-to-all(bf16[3,256,4,192]{1,3,0,2:T(8,128)(2,1)S(1)} %copy.122), channel_id=1, replica_groups=mesh['dp'=8,'seq'=4] {'seq'}, dimensions={2} | all-to-all | bytes 2359296 | tf_op jit(solution)/shard_map/all_to_all | solution.py:191
  443.9 81.4 %while.27 = (s32[]{:T(128)}, bf16[3,1024,3,64]{1,3,2,0:T(8,128)(2,1)}, bf16[3,1024,3,64]{1,3,2,0:T(8,128)(2,1)}, bf16[3,1024,3,64]{1,3,2,0:T(8,128)(2,1)}, bf16[...) while((s32[]{:T(128)}, ...), condition=%wide.region_14.15_spmd, body=%wide.region_12.14_spmd.sunk | while | flops 2062480384 | bytes 102610048 | solution.py:219
  536.4 44.7 %all-to-all-done.5 = bf16[3,1024,1,192]{3,0,2,1:T(4,128)(2,1)} async-done(((bf16[3,1024,1,192]{3,0,2,1:T(4,128)(2,1)}), bf16[3,1024,1,192]{3,0,2,1:T(4,128)(2,1)}, u32[]{:S(2)}, u32[]{:S(2)}) %all-to-all-start.5) | async-done | bytes 1179680 | tf_op jit(solution)/shard_map/all_to_all | solution.py:227
  598.0 35.8 %all-to-all-done.6 = bf16[3,1024,1,192]{3,0,2,1:T(4,128)(2,1)} async-done(((bf16[3,1024,1,192]{3,0,2,1:T(4,128)(2,1)}), bf16[3,1024,1,192]{3,0,2,1:T(4,128)(2,1)}, u32[]{:S(2)}, u32[]{:S(2)}) %all-to-all-start.6) | async-done | bytes 1179680 | tf_op jit(solution)/shard_map/all_to_all | solution.py:228
  699.2 7.8 fusion.173
  707.0 9.1 copy.134
  716.1 30.4 %concatenate.20 = f32[768,8,1152]{2,1,0:T(8,128)} concatenate(f32[768,8,288]{2,1,0:T(8,128)} %copy.134, f32[768,8,96]{2,1,0:T(8,128)S(1)} %copy-done.7, f32[768,8,384]{2,1,0:T(8,128)} %bitcast.278, f32[768,8,384]{2,1,0:T(8,128)} %bitcast.279), dimensions={2} | concatenate | bytes 56623104 | tf_op jit(solution)/shard_map/concatenate | solution.py:106
  746.5 25.3 %copy.155 = f32[96,8,8,1152]{3,1,2,0:T(8,128)} copy(f32[96,8,8,1152]{3,2,1,0:T(8,128)} %bitcast.271) | data formatting | bytes 56623104
  771.9 169.0 %reduce-scatter.3.cloned.1.call-done = f32[768,1152]{1,0:T(8,128)} async-done(((f32[768,9216]{1,0:T(8,128)}), f32[768,1152]{1,0:T(8,128)}) %reduce-scatter.3.cloned.1.call-update) | async-done | bytes 3538960 | tf_op jit(solution)/shard_map/reduce_scatter | solution.py:258
  944.3 75.6 %all-reduce.2.cloned.1.call-done = bf16[768,1152]{1,0:T(8,128)(2,1)} async-done(((bf16[768,1152]{1,0:T(8,128)(2,1)}), bf16[768,1152]{1,0:T(8,128)(2,1)}) %all-reduce.2.cloned.1.call-update) | async-done | bytes 1769488 | tf_op jit(solution)/shard_map/psum | solution.py:259
  1023.1 15.1 %fusion.77 = f32[768,2304]{0,1:T(8,128)} fusion(f32[288,768]{1,0:T(8,128)S(1)} %fusion.95, f32[1152,3072]{1,0:T(8,128)} %param.22), kind=kOutput, calls=%fused_computation.100 | convolution fusion | flops 6115295232 | bytes 10616832 | tf_op jit(solution)/shard_map/dot_general | solution.py:269
  1038.2 9.0 copy.137
  1060.5 17.9 %fusion.71 = f32[768,3072]{1,0:T(8,128)S(1)} fusion(f32[384,768]{1,0:T(8,128)S(1)} %fusion.87, f32[1152,3072]{1,0:T(8,128)} %param.22), kind=kOutput, calls=%fused_computation.91 | convolution fusion | flops 10871635968 | bytes 15335424 | tf_op jit(solution)/shard_map/dot_general | solution.py:269
  1087.8 17.7 %fusion.67 = f32[768,3072]{1,0:T(8,128)S(1)} fusion(f32[384,768]{1,0:T(8,128)S(1)} %fusion.83, f32[1152,3072]{1,0:T(8,128)} %param.22), kind=kOutput, calls=%fused_computation.87 | convolution fusion | flops 10871635968 | bytes 15335424 | tf_op jit(solution)/shard_map/dot_general | solution.py:269
  1111.2 30.4 %concatenate.21 = f32[768,8,1152]{2,1,0:T(8,128)} concatenate(f32[768,8,288]{2,1,0:T(8,128)} %copy.137, f32[768,8,96]{2,1,0:T(8,128)S(1)} %copy.138, f32[768,8,384]{2,1,0:T(8,128)} %bitcast.280, f32[768,8,384]{2,1,0:T(8,128)} %bitcast.281), dimensions={2} | concatenate | bytes 56623104 | tf_op jit(solution)/shard_map/concatenate | solution.py:106
  1141.6 25.3 %copy.158 = f32[96,8,8,1152]{3,1,2,0:T(8,128)} copy(f32[96,8,8,1152]{3,2,1,0:T(8,128)} %bitcast.272) | data formatting | bytes 56623104
  1167.2 169.6 %reduce-scatter.5.cloned.1.call-done = f32[768,1152]{1,0:T(8,128)} async-done(((f32[768,9216]{1,0:T(8,128)}), f32[768,1152]{1,0:T(8,128)}) %reduce-scatter.5.cloned.1.call-update) | async-done | bytes 3538960 | tf_op jit(solution)/shard_map/reduce_scatter | solution.py:271
  1336.8 8.2 add_divide_fusion
  1394.7 41.3 %psum.15 = f32[9216]{0:T(1024)} all-reduce(f32[9216]{0:T(1024)} %constant_dynamic-update-slice_fusion.6), channel_id=1, replica_groups=mesh['dp'=8,'seq'=4] {'dp','seq'}, use_global_device_ids=true, to_apply=%region_27.28 | all-reduce | flops 9216 | bytes 73728 | tf_op jit(solution)/shard_map/psum | solution.py:257
  1437.5 7.8 add_convert_fusion.1
  1453.0 8.3 fusion.167
  1465.6 9.4 fusion.65
  (303 shorter events, 456.6 us)
Async XLA Ops:
  7.2 84.9 %all-gather.3.cloned.1.call-start = ((), (), s32[]{:S(2)}) async-start(), calls=%async_computation.10 | async-start | bytes 15925248 | tf_op jit(solution)/shard_map/all_gather | solution.py:110
  122.7 33.5 %all-to-all-start = ((bf16[3,256,4,192]{1,3,0,2:T(8,128)(2,1)}), bf16[3,256,4,192]{1,3,0,2:T(8,128)(2,1)S(1)}, u32[]{:S(2)}, u32[]{:S(2)}) async-start(bf16[3,256,4,192]{1,3,0,2:T(8,128)(2,1)} %copy.113), calls=%async_computation | async-start | bytes 2359296 | tf_op jit(solution)/shard_map/all_to_all | solution.py:137
  156.2 32.5 %all-to-all-start.1 = ((bf16[3,256,4,192]{1,3,0,2:T(8,128)(2,1)}), bf16[3,256,4,192]{1,3,0,2:T(8,128)(2,1)}, u32[]{:S(2)}, u32[]{:S(2)}) async-start(bf16[3,256,4,192]{1,3,0,2:T(8,128)(2,1)} %copy.115), calls=%async_computation.1 | async-start | bytes 2359296 | tf_op jit(solution)/shard_map/all_to_all | solution.py:135
  188.7 32.0 %all-to-all-start.2 = ((bf16[3,256,4,192]{1,3,0,2:T(8,128)(2,1)}), bf16[3,256,4,192]{1,3,0,2:T(8,128)(2,1)S(1)}, u32[]{:S(2)}, u32[]{:S(2)}) async-start(bf16[3,256,4,192]{1,3,0,2:T(8,128)(2,1)} %copy.117), calls=%async_computation.2 | async-start | bytes 2359296 | tf_op jit(solution)/shard_map/all_to_all | solution.py:136
  276.1 52.4 %all-to-all-start.3 = ((bf16[3,1024,1,192]{3,0,2,1:T(4,128)(2,1)}), bf16[3,1024,1,192]{3,0,2,1:T(4,128)(2,1)}, u32[]{:S(2)}, u32[]{:S(2)}) async-start(bf16[3,1024,1,192]{3,0,2,1:T(4,128)(2,1)} %copy.119), calls=%async_computation.3 | async-start | bytes 4194304 | tf_op jit(solution)/shard_map/all_to_all | solution.py:160
  338.2 32.2 %slice-start.8 = ((s8[4718592]{0:T(1024)(128)(4,1)}), s8[4194304]{0:T(1024)(128)(4,1)S(1)}, s32[]{:S(2)}) async-start(s8[4718592]{0:T(1024)(128)(4,1)} %bitcast.313), calls=%async_computation.23 | async-start | bytes 8388608
  341.6 56.9 %copy-start.3 = (f32[768,768]{1,0:T(8,128)}, f32[768,768]{1,0:T(8,128)S(1)}, u32[]{:S(2)}) copy-start(f32[768,768]{1,0:T(8,128)S(1)} %get-tuple-element.239) | copy-start | bytes 7077892
  341.6 56.8 %copy-start.26 = (f32[768]{0:T(1024)}, f32[768]{0:T(1024)S(1)}, u32[]{:S(2)}) copy-start(f32[768]{0:T(1024)S(1)} %broadcast_multiply_fusion.5) | copy-start | bytes 9220
  342.0 56.4 %copy-start.30 = (f32[768]{0:T(1024)}, f32[768]{0:T(1024)S(1)}, u32[]{:S(2)}) copy-start(f32[768]{0:T(1024)S(1)} %add_rsqrt_fusion.1) | copy-start | bytes 9220
  342.1 28.3 %slice-start.9 = ((s8[4718592]{0:T(1024)(128)(4,1)}), s8[524288]{0:T(1024)(128)(4,1)S(1)}, s32[]{:S(2)}) async-start(s8[4718592]{0:T(1024)(128)(4,1)} %bitcast.313), calls=%async_computation.24 | async-start | bytes 1048576
  342.1 28.3 %copy-start.41 = (f32[768]{0:T(1024)S(1)}, f32[768]{0:T(1024)}, u32[]{:S(2)}) copy-start(f32[768]{0:T(1024)} %get-tuple-element.231) | copy-start | bytes 9220
  376.5 15.8 %slice-start.6 = ((s8[4718592]{0:T(1024)(128)(4,1)}), s8[524288]{0:T(1024)(128)(4,1)S(1)}, s32[]{:S(2)}) async-start(s8[4718592]{0:T(1024)(128)(4,1)} %bitcast.309), calls=%async_computation.21 | async-start | bytes 1048576
  379.0 13.2 slice-start.7
  529.4 51.7 %all-to-all-start.5 = ((bf16[3,1024,1,192]{3,0,2,1:T(4,128)(2,1)}), bf16[3,1024,1,192]{3,0,2,1:T(4,128)(2,1)}, u32[]{:S(2)}, u32[]{:S(2)}) async-start(bf16[3,1024,1,192]{3,0,2,1:T(4,128)(2,1)} %copy.124), calls=%async_computation.5 | async-start | bytes 4194304 | tf_op jit(solution)/shard_map/all_to_all | solution.py:227
  533.9 52.1 %copy-start.6 = (bf16[3,256,4,1,192]{4,2,1,0,3:T(4,128)(2,1)S(1)}, bf16[3,256,4,1,192]{4,2,1,0,3:T(4,128)(2,1)}, u32[]{:S(2)}) copy-start(bf16[3,256,4,1,192]{4,2,1,0,3:T(4,128)(2,1)} %copy-done.5) | copy-start | bytes 3538948
  581.1 52.7 %all-to-all-start.6 = ((bf16[3,1024,1,192]{3,0,2,1:T(4,128)(2,1)}), bf16[3,1024,1,192]{3,0,2,1:T(4,128)(2,1)}, u32[]{:S(2)}, u32[]{:S(2)}) async-start(bf16[3,1024,1,192]{3,0,2,1:T(4,128)(2,1)} %copy.127), calls=%async_computation.6 | async-start | bytes 4194304 | tf_op jit(solution)/shard_map/all_to_all | solution.py:228
  595.4 42.9 %copy-start.4 = (f32[768,768]{1,0:T(8,128)S(1)}, f32[768,768]{1,0:T(8,128)}, u32[]{:S(2)}) copy-start(f32[768,768]{1,0:T(8,128)} %copy-done.3) | copy-start | bytes 7077892
  595.4 42.9 %copy-start.27 = (f32[768]{0:T(1024)S(1)}, f32[768]{0:T(1024)}, u32[]{:S(2)}) copy-start(f32[768]{0:T(1024)} %copy-done.26) | copy-start | bytes 9220
  595.4 42.9 %copy-start.29 = (f32[768]{0:T(1024)S(1)}, f32[768]{0:T(1024)}, u32[]{:S(2)}) copy-start(f32[768]{0:T(1024)} %get-tuple-element.233) | copy-start | bytes 9220
  595.4 42.9 %copy-start.31 = (f32[768]{0:T(1024)S(1)}, f32[768]{0:T(1024)}, u32[]{:S(2)}) copy-start(f32[768]{0:T(1024)} %copy-done.30) | copy-start | bytes 9220
  595.4 42.9 %copy-start.33 = (f32[768]{0:T(1024)S(1)}, f32[768]{0:T(1024)}, u32[]{:S(2)}) copy-start(f32[768]{0:T(1024)} %get-tuple-element.232) | copy-start | bytes 9220
  633.8 52.3 %all-to-all-start.7 = ((bf16[3,1024,1,192]{3,0,2,1:T(4,128)(2,1)}), bf16[3,1024,1,192]{3,0,2,1:T(4,128)(2,1)}, u32[]{:S(2)}, u32[]{:S(2)}) async-start(bf16[3,1024,1,192]{3,0,2,1:T(4,128)(2,1)} %copy.130), calls=%async_computation.7 | async-start | bytes 4194304 | tf_op jit(solution)/shard_map/all_to_all | solution.py:229
  638.2 302.6 %reduce-scatter.3.cloned.1.call-start = ((), (), s32[]{:S(2)}) async-start(), calls=%async_computation.11 | async-start | bytes 31850496 | tf_op jit(solution)/shard_map/reduce_scatter | solution.py:258
  771.8 248.0 %all-reduce.2.cloned.1.call-start = ((), (), s32[]{:S(2)}) async-start(), calls=%async_computation.12 | async-start | bytes 3538944 | tf_op jit(solution)/shard_map/psum | solution.py:259
  944.2 392.6 %reduce-scatter.5.cloned.1.call-start = ((), (), s32[]{:S(2)}) async-start(), calls=%async_computation.13 | async-start | bytes 31850496 | tf_op jit(solution)/shard_map/reduce_scatter | solution.py:271
  1166.9 169.9 %copy-start.24 = (f32[768,1152]{1,0:T(8,128)S(1)}, f32[768,1152]{1,0:T(8,128)}, u32[]{:S(2)}) copy-start(f32[768,1152]{1,0:T(8,128)} %param.20) | copy-start | bytes 10616836
  1166.9 286.1 %all-gather.5.cloned.1.call-start = ((), (), s32[]{:S(2)}) async-start(), calls=%async_computation.14 | async-start | bytes 15925248 | tf_op jit(solution)/shard_map/all_gather | solution.py:284
  1373.0 17.8 %copy-start.39 = (f32[768]{0:T(1024)S(1)}, f32[768]{0:T(1024)}, u32[]{:S(2)}) copy-start(f32[768]{0:T(1024)} %get-tuple-element.210) | copy-start | bytes 9220
  1373.0 19.1 %copy-start.38 = (f32[768]{0:T(1024)S(1)}, f32[768]{0:T(1024)}, u32[]{:S(2)}) copy-start(f32[768]{0:T(1024)} %get-tuple-element.208) | copy-start | bytes 9220
  1453.0 22.0 %slice-start = ((s8[14155776]{0:T(1024)(128)(4,1)}), s8[1572864]{0:T(1024)(128)(4,1)S(1)}, s32[]{:S(2)}) async-start(s8[14155776]{0:T(1024)(128)(4,1)} %bitcast.290), calls=%async_computation.15 | async-start | bytes 3145728
  1453.0 22.0 %slice-start.1 = ((s8[14155776]{0:T(1024)(128)(4,1)}), s8[4194304]{0:T(1024)(128)(4,1)S(1)}, s32[]{:S(2)}) async-start(s8[14155776]{0:T(1024)(128)(4,1)} %bitcast.290), calls=%async_computation.16 | async-start | bytes 8388608
  1461.4 13.7 slice-start.2
  (39 other events, 228.1 us)
Sparse Core Ops, SparseCore 0:
  10.8 81.2 all-gather.2
  771.9 168.8 reduce-scatter.2
  944.4 75.4 all-reduce.1
  1167.1 169.7 reduce-scatter.4
  1373.1 79.8 all-gather.4
where the time goes:
time: 1520 us; the launch traced here: 1510 us
  waiting for transfers between devices  686 us (45%)
  local copies, waits for them, and re-layouts  334 us (22%)
  matrix products  287 us (19%)
  other arithmetic  80 us (5%)
  blocking collectives  72 us (5%)
  starting transfers between devices  31.7 us (2%)
    reduce_scatter x1, waiting for transfers between devices, on_device(): rotated = lax.psum_scatter(term, 'dp', scatter_dimension=1, tiled=True)  170 us
    reduce_scatter x1, waiting for transfers between devices, on_device(): reduced = lax.psum_scatter(grad_full, 'dp', scatter_dimension=1, tiled=True)  169 us
    unnamed x130, local copies, waits for them, and re-layouts  100 us
    all_gather x1, waiting for transfers between devices, on_device(): lax.all_gather(weights.astype(jnp.bfloat16), 'dp', axis=1, tiled=True)  80.8 us
    psum x1, waiting for transfers between devices, on_device(): reduced = lax.psum(reduced.astype(jnp.bfloat16), 'seq').astype(jnp.float32)  75.6 us
    concatenate x2, local copies, waits for them, and re-layouts, join_wide(): jnp.concatenate([parts[which].reshape(rows, owners, block_widths[which])...  60.8 us
    dot_general x4, matrix products, on_device(): turned_parts.append(jnp.dot(left_turned, rows_here, precision=highest))  55.1 us
    all_to_all x1, waiting for transfers between devices, on_device(): lax.all_to_all(to_send(grads_q), 'seq', split_axis=1, concat_axis=2, tile...  44.7 us
  transfers between devices with their start and end apart: 12, of which 12 were waited for; matrix products, arithmetic and copies ran while one was open for 8% of the time, Pallas kernels for 0%

commit v1 on v0

--- a/solution.py
+++ b/solution.py
@@ -256,7 +256,8 @@
     )
     small_grad = lax.psum(small_local, ("dp", "seq"))
     reduced = lax.psum_scatter(grad_full, "dp", scatter_dimension=1, tiled=True)
-    reduced = lax.psum(reduced.astype(jnp.bfloat16), "seq").astype(jnp.float32)
+    racks_arrange = lambda original, group_axis: jnp.sum(lax.all_gather(original, group_axis), 0)
+    reduced = racks_arrange(reduced.astype(jnp.bfloat16), "seq").astype(jnp.float32)
     right_rows = []
     turned_parts = []
     for which in range(4):

time: 1520 us -> 1580 us (1.039)
  waiting for transfers between devices: 686 us -> 752 us
    all_gather x0 -> x1, waiting for transfers between devices: none -> 128 us  [on_device(): lax.all_gather(original, group_axis)]
    psum x1 -> x0, waiting for transfers between devices: 75.6 us -> none  [on_device(): reduced = lax.psum(reduced.astype(jnp.bfloat16), 'seq').astype(jnp.float32)]
    unnamed x130 -> x142, local copies, waits for them, and re-layouts: 100 us -> 92.7 us
  transfers between devices with their start and end apart: 12 -> 12, of which waited for: 12 -> 12; matrix products, arithmetic and copies ran while one was open for 8% -> 7% of each run, Pallas kernels for 0% -> 0%
where the time goes in v1:
time: 1580 us; the launch traced here: 1570 us
  waiting for transfers between devices  752 us (48%)
  local copies, waits for them, and re-layouts  325 us (21%)
  matrix products  288 us (18%)
  other arithmetic  82 us (5%)
  blocking collectives  71.7 us (5%)
  starting transfers between devices  31.6 us (2%)
    reduce_scatter x1, waiting for transfers between devices, on_device(): reduced = lax.psum_scatter(grad_full, 'dp', scatter_dimension=1, tiled=True)  169 us
    reduce_scatter x1, waiting for transfers between devices, on_device(): rotated = lax.psum_scatter(term, 'dp', scatter_dimension=1, tiled=True)  169 us
    all_gather x1, waiting for transfers between devices, on_device(): lax.all_gather(original, group_axis)  128 us
    unnamed x142, local copies, waits for them, and re-layouts  92.7 us
    all_gather x1, waiting for transfers between devices, on_device(): lax.all_gather(weights.astype(jnp.bfloat16), 'dp', axis=1, tiled=True)  80.8 us
    concatenate x2, local copies, waits for them, and re-layouts, join_wide(): jnp.concatenate([parts[which].reshape(rows, owners, block_widths[which])...  61.4 us
    dot_general x4, matrix products, on_device(): turned_parts.append(jnp.dot(left_turned, rows_here, precision=highest))  55.5 us
    all_to_all x1, waiting for transfers between devices, on_device(): lax.all_to_all(to_send(grads_q), 'seq', split_axis=1, concat_axis=2, tile...  44.8 us
  transfers between devices with their start and end apart: 12, of which 12 were waited for; matrix products, arithmetic and copies ran while one was open for 7% of the time, Pallas kernels for 0%

profile of v1, /device:TPU:0, one launch (start us, length us, event | category | flops | bytes accessed | tf_op | source)
XLA Modules:
  0.0 1565.8 jit_solution(12672901740985369222)
XLA Ops:
  11.3 80.8 %all-gather.5.cloned.1.call-done = bf16[768,9216]{1,0:T(8,128)(2,1)} async-done(((bf16[768,1152]{1,0:T(8,128)(2,1)}), bf16[768,9216]{1,0:T(8,128)(2,1)}) %all-gather.5.cloned.1.call-update) | async-done | bytes 14155792 | tf_op jit(solution)/shard_map/all_gather | solution.py:110
  92.1 18.6 %copy.112 = bf16[768,9216]{0,1:T(8,128)(2,1)} copy(bf16[768,9216]{1,0:T(8,128)(2,1)} %all-gather.5.cloned.1.call-done) | data formatting | bytes 28311552 | tf_op jit(solution)/shard_map/all_gather | solution.py:110
  132.9 23.3 %all-to-all-done = bf16[3,256,4,192]{1,3,0,2:T(8,128)(2,1)S(1)} async-done(((bf16[3,256,4,192]{1,3,0,2:T(8,128)(2,1)}), bf16[3,256,4,192]{1,3,0,2:T(8,128)(2,1)S(1)}, u32[]{:S(2)}, u32[]{:S(2)}) %all-to-all-start) | async-done | bytes 1179680 | tf_op jit(solution)/shard_map/all_to_all | solution.py:137
  169.0 19.7 %all-to-all-done.1 = bf16[3,256,4,192]{1,3,0,2:T(8,128)(2,1)} async-done(((bf16[3,256,4,192]{1,3,0,2:T(8,128)(2,1)}), bf16[3,256,4,192]{1,3,0,2:T(8,128)(2,1)}, u32[]{:S(2)}, u32[]{:S(2)}) %all-to-all-start.1) | async-done | bytes 1179680 | tf_op jit(solution)/shard_map/all_to_all | solution.py:135
  201.9 18.9 %all-to-all-done.2 = bf16[3,256,4,192]{1,3,0,2:T(8,128)(2,1)S(1)} async-done(((bf16[3,256,4,192]{1,3,0,2:T(8,128)(2,1)}), bf16[3,256,4,192]{1,3,0,2:T(8,128)(2,1)S(1)}, u32[]{:S(2)}, u32[]{:S(2)}) %all-to-all-start.2) | async-done | bytes 1179680 | tf_op jit(solution)/shard_map/all_to_all | solution.py:136
  224.5 47.5 %while.26 = (s32[]{:T(128)}, bf16[3,1024,3,64]{1,3,2,0:T(8,128)(2,1)}, f32[3,3,1024,1]{2,1,3,0:T(4,128)}, bf16[3,1024,3,64]{1,3,2,0:T(8,128)(2,1)}, s32[3,1024]{...) while((s32[]{:T(128)}, ...), condition=%wide.region_3.4_spmd, body=%wide.region_0.3_spmd.sunk | while | flops 844297216 | bytes 47827072 | solution.py:158
  285.0 8.2 fusion.168
  293.2 35.4 %all-to-all-done.3 = bf16[3,1024,1,192]{3,0,2,1:T(4,128)(2,1)} async-done(((bf16[3,1024,1,192]{3,0,2,1:T(4,128)(2,1)}), bf16[3,1024,1,192]{3,0,2,1:T(4,128)(2,1)}, u32[]{:S(2)}, u32[]{:S(2)}) %all-to-all-start.3) | async-done | bytes 1179680 | tf_op jit(solution)/shard_map/all_to_all | solution.py:160
  342.1 28.3 %multiply_convert_fusion.1 = (bf16[768,3072]{1,0:T(8,128)(2,1)S(1)}, f32[768,3072]{1,0:T(8,128)}, f32[768,3072]{1,0:T(8,128)}) fusion(f32[3072]{0:T(1024)S(1)} %slice.124, bf16[768,3072]{0,1:T(8,128)(2,1)} %bitcast.310, f32[768,768]{1,0:T(8,128)S(1)} %get-tuple-element.239, f32[768]{0:T(1024)S(1)} %copy-done.31, f32[768]{0:T(1024)S(1)} %copy-done.27, ...), kind=kOutput, calls=%fused_computation.70 | convolution fusion | flops 3782541312 | bytes 30695424 | tf_op jit(solution)/shard_map/dot_general | solution.py:166
  379.1 13.2 convert_reduce_fusion
  405.0 30.7 %all_to_all.120 = bf16[3,256,4,192]{1,3,0,2:T(8,128)(2,1)S(1)} all-to-all(bf16[3,256,4,192]{1,3,0,2:T(8,128)(2,1)S(1)} %copy.122), channel_id=1, replica_groups=mesh['dp'=8,'seq'=4] {'seq'}, dimensions={2} | all-to-all | bytes 2359296 | tf_op jit(solution)/shard_map/all_to_all | solution.py:191
  443.9 81.4 %while.27 = (s32[]{:T(128)}, bf16[3,1024,3,64]{1,3,2,0:T(8,128)(2,1)}, bf16[3,1024,3,64]{1,3,2,0:T(8,128)(2,1)}, bf16[3,1024,3,64]{1,3,2,0:T(8,128)(2,1)}, bf16[...) while((s32[]{:T(128)}, ...), condition=%wide.region_14.15_spmd, body=%wide.region_12.14_spmd.sunk | while | flops 2062480384 | bytes 102610048 | solution.py:219
  536.4 44.8 %all-to-all-done.5 = bf16[3,1024,1,192]{3,0,2,1:T(4,128)(2,1)} async-done(((bf16[3,1024,1,192]{3,0,2,1:T(4,128)(2,1)}), bf16[3,1024,1,192]{3,0,2,1:T(4,128)(2,1)}, u32[]{:S(2)}, u32[]{:S(2)}) %all-to-all-start.5) | async-done | bytes 1179680 | tf_op jit(solution)/shard_map/all_to_all | solution.py:227
  597.8 35.8 %all-to-all-done.6 = bf16[3,1024,1,192]{3,0,2,1:T(4,128)(2,1)} async-done(((bf16[3,1024,1,192]{3,0,2,1:T(4,128)(2,1)}), bf16[3,1024,1,192]{3,0,2,1:T(4,128)(2,1)}, u32[]{:S(2)}, u32[]{:S(2)}) %all-to-all-start.6) | async-done | bytes 1179680 | tf_op jit(solution)/shard_map/all_to_all | solution.py:228
  706.8 9.1 copy.134
  715.9 30.4 %concatenate.20 = f32[768,8,1152]{2,1,0:T(8,128)} concatenate(f32[768,8,288]{2,1,0:T(8,128)} %copy.134, f32[768,8,96]{2,1,0:T(8,128)S(1)} %copy-done.8, f32[768,8,384]{2,1,0:T(8,128)} %bitcast.279, f32[768,8,384]{2,1,0:T(8,128)} %bitcast.280), dimensions={2} | concatenate | bytes 56623104 | tf_op jit(solution)/shard_map/concatenate | solution.py:106
  746.3 25.3 %copy.155 = f32[96,8,8,1152]{3,1,2,0:T(8,128)} copy(f32[96,8,8,1152]{3,2,1,0:T(8,128)} %bitcast.272) | data formatting | bytes 56623104
  771.7 168.9 %reduce-scatter.3.cloned.1.call-done = f32[768,1152]{1,0:T(8,128)} async-done(((f32[768,9216]{1,0:T(8,128)}), f32[768,1152]{1,0:T(8,128)}) %reduce-scatter.3.cloned.1.call-update) | async-done | bytes 3538960 | tf_op jit(solution)/shard_map/reduce_scatter | solution.py:258
  944.3 128.1 %all-gather.9.cloned.1.call-done = bf16[3072,1152]{1,0:T(8,128)(2,1)} async-done(((bf16[768,1152]{1,0:T(8,128)(2,1)}), bf16[3072,1152]{1,0:T(8,128)(2,1)}) %all-gather.9.cloned.1.call-update) | async-done | bytes 7077904 | tf_op jit(solution)/shard_map/all_gather | solution.py:259
  1091.1 15.1 fusion.77
  1106.2 9.0 copy.137
  1123.0 18.3 %fusion.71 = f32[768,3072]{1,0:T(8,128)S(1)} fusion(f32[384,768]{1,0:T(8,128)} %fusion.87, f32[1152,3072]{1,0:T(8,128)} %param.22), kind=kOutput, calls=%fused_computation.91 | convolution fusion | flops 10871635968 | bytes 15335424 | tf_op jit(solution)/shard_map/dot_general | solution.py:270
  1147.1 17.7 %fusion.67 = f32[768,3072]{1,0:T(8,128)S(1)} fusion(f32[384,768]{1,0:T(8,128)S(1)} %fusion.83, f32[1152,3072]{1,0:T(8,128)} %param.22), kind=kOutput, calls=%fused_computation.87 | convolution fusion | flops 10871635968 | bytes 15335424 | tf_op jit(solution)/shard_map/dot_general | solution.py:270
  1170.6 31.0 %concatenate.21 = f32[768,8,1152]{2,1,0:T(8,128)} concatenate(f32[768,8,288]{2,1,0:T(8,128)} %copy.137, f32[768,8,96]{2,1,0:T(8,128)} %copy.138, f32[768,8,384]{2,1,0:T(8,128)} %bitcast.281, f32[768,8,384]{2,1,0:T(8,128)} %bitcast.282), dimensions={2} | concatenate | bytes 56623104 | tf_op jit(solution)/shard_map/concatenate | solution.py:106
  1201.6 25.3 %copy.158 = f32[96,8,8,1152]{3,1,2,0:T(8,128)} copy(f32[96,8,8,1152]{3,2,1,0:T(8,128)} %bitcast.273) | data formatting | bytes 56623104
  1227.2 168.8 %reduce-scatter.5.cloned.1.call-done = f32[768,1152]{1,0:T(8,128)} async-done(((f32[768,9216]{1,0:T(8,128)}), f32[768,1152]{1,0:T(8,128)}) %reduce-scatter.5.cloned.1.call-update) | async-done | bytes 3538960 | tf_op jit(solution)/shard_map/reduce_scatter | solution.py:272
  1396.0 9.2 add_divide_fusion
  1441.6 41.0 %psum.7 = f32[9216]{0:T(1024)S(1)} all-reduce(f32[9216]{0:T(1024)S(1)} %constant_dynamic-update-slice_fusion.6), channel_id=1, replica_groups=mesh['dp'=8,'seq'=4] {'dp','seq'}, use_global_device_ids=true, to_apply=%region_27.28 | all-reduce | flops 9216 | bytes 73728 | tf_op jit(solution)/shard_map/psum | solution.py:257
  1483.3 7.8 add_convert_fusion.1
  1493.1 20.2 %all-gather.7.cloned.1.call-done = bf16[768,9216]{0,1:T(8,128)(2,1)} async-done(((bf16[768,1152]{0,1:T(8,128)(2,1)}), bf16[768,9216]{0,1:T(8,128)(2,1)}) %all-gather.7.cloned.1.call-update) | async-done | bytes 14155792 | tf_op jit(solution)/shard_map/all_gather | solution.py:285
  1513.3 8.3 fusion.167
  1525.9 10.1 fusion.65
  (316 shorter events, 449.1 us)
Async XLA Ops:
  7.2 84.9 %all-gather.5.cloned.1.call-start = ((), (), s32[]{:S(2)}) async-start(), calls=%async_computation.10 | async-start | bytes 15925248 | tf_op jit(solution)/shard_map/all_gather | solution.py:110
  122.7 33.6 %all-to-all-start = ((bf16[3,256,4,192]{1,3,0,2:T(8,128)(2,1)}), bf16[3,256,4,192]{1,3,0,2:T(8,128)(2,1)S(1)}, u32[]{:S(2)}, u32[]{:S(2)}) async-start(bf16[3,256,4,192]{1,3,0,2:T(8,128)(2,1)} %copy.113), calls=%async_computation | async-start | bytes 2359296 | tf_op jit(solution)/shard_map/all_to_all | solution.py:137
  156.3 32.4 %all-to-all-start.1 = ((bf16[3,256,4,192]{1,3,0,2:T(8,128)(2,1)}), bf16[3,256,4,192]{1,3,0,2:T(8,128)(2,1)}, u32[]{:S(2)}, u32[]{:S(2)}) async-start(bf16[3,256,4,192]{1,3,0,2:T(8,128)(2,1)} %copy.115), calls=%async_computation.1 | async-start | bytes 2359296 | tf_op jit(solution)/shard_map/all_to_all | solution.py:135
  188.7 32.0 %all-to-all-start.2 = ((bf16[3,256,4,192]{1,3,0,2:T(8,128)(2,1)}), bf16[3,256,4,192]{1,3,0,2:T(8,128)(2,1)S(1)}, u32[]{:S(2)}, u32[]{:S(2)}) async-start(bf16[3,256,4,192]{1,3,0,2:T(8,128)(2,1)} %copy.117), calls=%async_computation.2 | async-start | bytes 2359296 | tf_op jit(solution)/shard_map/all_to_all | solution.py:136
  276.1 52.5 %all-to-all-start.3 = ((bf16[3,1024,1,192]{3,0,2,1:T(4,128)(2,1)}), bf16[3,1024,1,192]{3,0,2,1:T(4,128)(2,1)}, u32[]{:S(2)}, u32[]{:S(2)}) async-start(bf16[3,1024,1,192]{3,0,2,1:T(4,128)(2,1)} %copy.119), calls=%async_computation.3 | async-start | bytes 4194304 | tf_op jit(solution)/shard_map/all_to_all | solution.py:160
  338.3 32.2 %slice-start.8 = ((s8[4718592]{0:T(1024)(128)(4,1)}), s8[4194304]{0:T(1024)(128)(4,1)S(1)}, s32[]{:S(2)}) async-start(s8[4718592]{0:T(1024)(128)(4,1)} %bitcast.315), calls=%async_computation.23 | async-start | bytes 8388608
  341.6 56.9 %copy-start.3 = (f32[768,768]{1,0:T(8,128)}, f32[768,768]{1,0:T(8,128)S(1)}, u32[]{:S(2)}) copy-start(f32[768,768]{1,0:T(8,128)S(1)} %get-tuple-element.239) | copy-start | bytes 7077892
  341.7 56.8 %copy-start.25 = (f32[768]{0:T(1024)}, f32[768]{0:T(1024)S(1)}, u32[]{:S(2)}) copy-start(f32[768]{0:T(1024)S(1)} %broadcast_multiply_fusion.5) | copy-start | bytes 9220
  342.1 56.4 %copy-start.29 = (f32[768]{0:T(1024)}, f32[768]{0:T(1024)S(1)}, u32[]{:S(2)}) copy-start(f32[768]{0:T(1024)S(1)} %add_rsqrt_fusion.1) | copy-start | bytes 9220
  342.1 28.3 %slice-start.9 = ((s8[4718592]{0:T(1024)(128)(4,1)}), s8[524288]{0:T(1024)(128)(4,1)S(1)}, s32[]{:S(2)}) async-start(s8[4718592]{0:T(1024)(128)(4,1)} %bitcast.315), calls=%async_computation.24 | async-start | bytes 1048576
  342.1 28.3 %copy-start.46 = (f32[768]{0:T(1024)S(1)}, f32[768]{0:T(1024)}, u32[]{:S(2)}) copy-start(f32[768]{0:T(1024)} %get-tuple-element.231) | copy-start | bytes 9220
  376.5 15.8 %slice-start.6 = ((s8[4718592]{0:T(1024)(128)(4,1)}), s8[524288]{0:T(1024)(128)(4,1)S(1)}, s32[]{:S(2)}) async-start(s8[4718592]{0:T(1024)(128)(4,1)} %bitcast.311), calls=%async_computation.21 | async-start | bytes 1048576
  379.1 13.2 slice-start.7
  529.4 51.7 %all-to-all-start.5 = ((bf16[3,1024,1,192]{3,0,2,1:T(4,128)(2,1)}), bf16[3,1024,1,192]{3,0,2,1:T(4,128)(2,1)}, u32[]{:S(2)}, u32[]{:S(2)}) async-start(bf16[3,1024,1,192]{3,0,2,1:T(4,128)(2,1)} %copy.124), calls=%async_computation.5 | async-start | bytes 4194304 | tf_op jit(solution)/shard_map/all_to_all | solution.py:227
  533.9 51.9 %copy-start.7 = (bf16[3,256,4,1,192]{4,2,1,0,3:T(4,128)(2,1)S(1)}, bf16[3,256,4,1,192]{4,2,1,0,3:T(4,128)(2,1)}, u32[]{:S(2)}) copy-start(bf16[3,256,4,1,192]{4,2,1,0,3:T(4,128)(2,1)} %copy-done.6) | copy-start | bytes 3538948
  581.2 52.5 %all-to-all-start.6 = ((bf16[3,1024,1,192]{3,0,2,1:T(4,128)(2,1)}), bf16[3,1024,1,192]{3,0,2,1:T(4,128)(2,1)}, u32[]{:S(2)}, u32[]{:S(2)}) async-start(bf16[3,1024,1,192]{3,0,2,1:T(4,128)(2,1)} %copy.127), calls=%async_computation.6 | async-start | bytes 4194304 | tf_op jit(solution)/shard_map/all_to_all | solution.py:228
  595.2 42.9 %copy-start.4 = (f32[768,768]{1,0:T(8,128)S(1)}, f32[768,768]{1,0:T(8,128)}, u32[]{:S(2)}) copy-start(f32[768,768]{1,0:T(8,128)} %copy-done.3) | copy-start | bytes 7077892
  595.2 42.9 %copy-start.26 = (f32[768]{0:T(1024)S(1)}, f32[768]{0:T(1024)}, u32[]{:S(2)}) copy-start(f32[768]{0:T(1024)} %copy-done.25) | copy-start | bytes 9220
  595.2 42.9 %copy-start.28 = (f32[768]{0:T(1024)S(1)}, f32[768]{0:T(1024)}, u32[]{:S(2)}) copy-start(f32[768]{0:T(1024)} %get-tuple-element.233) | copy-start | bytes 9220
  595.2 42.9 %copy-start.30 = (f32[768]{0:T(1024)S(1)}, f32[768]{0:T(1024)}, u32[]{:S(2)}) copy-start(f32[768]{0:T(1024)} %copy-done.29) | copy-start | bytes 9220
  595.2 42.9 %copy-start.32 = (f32[768]{0:T(1024)S(1)}, f32[768]{0:T(1024)}, u32[]{:S(2)}) copy-start(f32[768]{0:T(1024)} %get-tuple-element.232) | copy-start | bytes 9220
  633.6 52.3 %all-to-all-start.7 = ((bf16[3,1024,1,192]{3,0,2,1:T(4,128)(2,1)}), bf16[3,1024,1,192]{3,0,2,1:T(4,128)(2,1)}, u32[]{:S(2)}, u32[]{:S(2)}) async-start(bf16[3,1024,1,192]{3,0,2,1:T(4,128)(2,1)} %copy.130), calls=%async_computation.7 | async-start | bytes 4194304 | tf_op jit(solution)/shard_map/all_to_all | solution.py:229
  638.1 302.5 %reduce-scatter.3.cloned.1.call-start = ((), (), s32[]{:S(2)}) async-start(), calls=%async_computation.11 | async-start | bytes 31850496 | tf_op jit(solution)/shard_map/reduce_scatter | solution.py:258
  771.6 300.7 %all-gather.9.cloned.1.call-start = ((), (), s32[]{:S(2)}) async-start(), calls=%async_computation.14 | async-start | bytes 8847360 | tf_op jit(solution)/shard_map/all_gather | solution.py:259
  944.0 452.0 %reduce-scatter.5.cloned.1.call-start = ((), (), s32[]{:S(2)}) async-start(), calls=%async_computation.12 | async-start | bytes 31850496 | tf_op jit(solution)/shard_map/reduce_scatter | solution.py:272
  1227.0 286.4 %all-gather.7.cloned.1.call-start = ((), (), s32[]{:S(2)}) async-start(), calls=%async_computation.13 | async-start | bytes 15925248 | tf_op jit(solution)/shard_map/all_gather | solution.py:285
  1433.3 49.3 %copy-start.34 = (f32[9216]{0:T(1024)S(1)}, f32[9216]{0:T(1024)}, u32[]{:S(2)}) copy-start(f32[9216]{0:T(1024)} %param.23) | copy-start | bytes 110596
  1433.3 49.3 %copy-start.38 = (f32[9216]{0:T(1024)S(1)}, f32[9216]{0:T(1024)}, u32[]{:S(2)}) copy-start(f32[9216]{0:T(1024)} %param.25) | copy-start | bytes 110596
  1433.3 49.3 %copy-start.39 = (f32[9216]{0:T(1024)S(1)}, f32[9216]{0:T(1024)}, u32[]{:S(2)}) copy-start(f32[9216]{0:T(1024)} %param.24) | copy-start | bytes 110596
  1513.3 22.8 %slice-start = ((s8[14155776]{0:T(1024)(128)(4,1)}), s8[1572864]{0:T(1024)(128)(4,1)S(1)}, s32[]{:S(2)}) async-start(s8[14155776]{0:T(1024)(128)(4,1)} %bitcast.291), calls=%async_computation.15 | async-start | bytes 3145728
  1513.3 22.8 %slice-start.1 = ((s8[14155776]{0:T(1024)(128)(4,1)}), s8[4194304]{0:T(1024)(128)(4,1)S(1)}, s32[]{:S(2)}) async-start(s8[14155776]{0:T(1024)(128)(4,1)} %bitcast.291), calls=%async_computation.16 | async-start | bytes 8388608
  1521.6 14.4 slice-start.2
  (45 other events, 272.9 us)
Sparse Core Ops, SparseCore 0:
  10.8 81.2 all-gather.4
  771.8 168.8 reduce-scatter.2
  944.2 128.1 all-gather.8
  1227.1 168.8 reduce-scatter.4
  1433.3 79.9 all-gather.6
